TPU v7x, 32 devices: a whole 2x2x4 slice. The times are simulated.
32 devices in a mesh: shot: 4 (over x, core), gx: 2 (over y), gy: 4 (over z).
Axes of the slice: x: 2, y: 2, z: 4, core: 2. Of those that a mesh axis runs over, the one named last changes fastest.
Arguments:
- state_now: float32 [4, 16, 256, 256], P('shot', 'gx', 'gy'), may hold values from -6 to 6
- state_prev: float32 [4, 16, 256, 256], P('shot', 'gx', 'gy'), may hold values from -6 to 6
- courant_sq: float32 [16, 256, 256], P('gx', 'gy'), may hold values from 0.03 to 0.3
- reflectivity: float32 [16, 256, 256], P('gx', 'gy'), may hold values from -6 to 6
- direction: float32 [16, 256, 256], P('gx', 'gy'), may hold values from -6 to 6
- prev_gradient: float32 [16, 256, 256], P('gx', 'gy'), may hold values from -3 to 3
- residual: float32 [4, 16, 16, 256], P('shot', None, 'gx', 'gy'), may hold values from -6 to 6
- rec_depth: int32 [4, 16, 256], P('shot', 'gx', 'gy'), may hold values from 0 to 255
- source_cell: int32 [4, 3], P('shot'), may hold values from 0 to 255, as said below
- wavelet: float32 [4, 15], P('shot'), may hold values from -80 to 80
- live_steps: int32 [4], P('shot'), may hold values from 8 to 16
Outputs:
- image_next: float32 [16, 256, 256], P('gx', 'gy')
- direction_next: float32 [16, 256, 256], P('gx', 'gy')
- residual_next: float32 [4, 16, 16, 256], P('shot', None, 'gx', 'gy')
- data_misfit: float32 [], replicated
Inputs may be any that keep to these rules, and one draw needn't show every extreme that they name: `source_cell`: column 0 lies in 0 to 15, column 1 in 0 to 255, column 2 in 0 to 255.
All inputs are finite; a program needn't handle non-finite values.
Results may differ from a plain program's by a relative error of at most 0.0003.
Values sent between devices are 32-bit elements; how exact they have to be, the bound alone decides.
A program may use at most 64 MiB of HBM per device.

v0:
```python
import jax
import jax.numpy as jnp
from jax import lax
from jax.sharding import PartitionSpec as P


def with_halo(array, sides, width):
    for axis, dim in sides:
        size, length = (lax.axis_size(axis), array.shape[dim])
        up = [(i, (i + 1) % size) for i in range(size - 1)]
        down = [(j, i) for i, j in up]
        last = lax.slice_in_dim(array, length - width, length, axis=dim)
        first = lax.slice_in_dim(array, 0, width, axis=dim)
        before = lax.ppermute(last, axis, up)
        after = lax.ppermute(first, axis, down)
        array = jnp.concatenate([before, array, after], axis=dim)
    return array


def neighbours(padded, values):
    inner = padded[:, 2:, 1:-1] + padded[:, :-2, 1:-1] + padded[:, 1:-1, 2:] + padded[:, 1:-1, :-2]
    deeper = jnp.pad(values, ((0, 0), (0, 0), (0, 0), (1, 1)))
    inner = inner + deeper[:, :, :, 2:] + deeper[:, :, :, :-2]
    return inner - 6.0 * values


def on_device(
    state_now,
    state_prev,
    courant_sq,
    reflectivity,
    direction,
    prev_gradient,
    residual,
    rec_depth,
    source_cell,
    wavelet,
    live_steps,
):
    shot_count, extent_x, extent_y, extent_z = state_now.shape
    step_count = residual.shape[1]
    global_x = lax.axis_index("gx") * extent_x + lax.iota(jnp.int32, extent_x)
    global_y = lax.axis_index("gy") * extent_y + lax.iota(jnp.int32, extent_y)
    depth_axis = lax.iota(jnp.int32, extent_z)
    spot = (
        (global_x[None, :, None, None] == source_cell[:, 0, None, None, None])
        & (global_y[None, None, :, None] == source_cell[:, 1, None, None, None])
        & (depth_axis[None, None, None, :] == source_cell[:, 2, None, None, None])
    ).astype(jnp.float32)
    receivers = (depth_axis[None, None, None, :] == rec_depth[:, :, :, None]).astype(jnp.float32)
    live_mask = (lax.iota(jnp.int32, step_count)[None, :] < live_steps[:, None]).astype(jnp.float32)
    weighted = residual * live_mask[:, :, None, None]
    stored = jnp.zeros((step_count,) + state_now.shape, jnp.float32)
    stored = lax.dynamic_update_index_in_dim(stored, state_now, 0, 0)

    def advance(index, carry):
        present, former, history = carry
        padded = with_halo(present, (("gx", 1), ("gy", 2)), 1)
        amplitude = lax.dynamic_index_in_dim(wavelet, index, 1, keepdims=False)
        advanced = (
            2.0 * present
            - former
            + courant_sq * neighbours(padded, present)
            + amplitude[:, None, None, None] * spot
        )
        history = lax.dynamic_update_index_in_dim(history, advanced, index + 1, 0)
        return (advanced, present, history)

    unused_a, unused_b, stored = lax.fori_loop(
        0, step_count - 1, advance, (state_now, state_prev, stored)
    )
    newest = receivers * weighted[:, step_count - 1, :, :, None]
    accumulated = stored[step_count - 1] * newest

    def retreat(offset, carry):
        following, furthest, summed = carry
        index = step_count - 2 - offset
        scaled = courant_sq * following
        padded = with_halo(scaled, (("gx", 1), ("gy", 2)), 1)
        weight = lax.dynamic_index_in_dim(weighted, index, 1, keepdims=False)
        current = (
            2.0 * following
            - furthest
            + neighbours(padded, scaled)
            + receivers * weight[:, :, :, None]
        )
        wavefield = lax.dynamic_index_in_dim(stored, index, 0, keepdims=False)
        return (current, following, summed + wavefield * current)

    unused_c, unused_d, accumulated = lax.fori_loop(
        0, step_count - 1, retreat, (newest, jnp.zeros_like(newest), accumulated)
    )
    local_gradient = courant_sq * jnp.sum(accumulated, axis=0)
    quarter = extent_z // lax.axis_size("shot")
    offset_z = lax.axis_index("shot") * quarter

    def share(values):
        return lax.dynamic_slice_in_dim(values, offset_z, quarter, 2)

    gradient = lax.psum(local_gradient, "shot")
    grad_share = share(gradient)
    old_share = share(prev_gradient)
    path_share = share(direction)
    partials = (
        jnp.sum(grad_share * grad_share),
        jnp.sum(grad_share * old_share),
        jnp.sum(old_share * old_share),
    )
    partials = partials + (jnp.sum(grad_share * path_share),)
    summed = lax.psum(partials, ("shot", "gx", "gy"))
    beta_coef = (summed[0] - summed[1]) / summed[2]
    direction_next = gradient + beta_coef * direction
    slope = summed[0] + beta_coef * summed[3]
    gain = courant_sq * direction_next
    first_wave = gain * stored[0]
    records = jnp.zeros(residual.shape, jnp.float32)
    first_record = jnp.sum(receivers * first_wave, axis=3) * live_mask[:, 0, None, None]
    records = lax.dynamic_update_index_in_dim(records, first_record, 0, 1)

    def propagate(index, carry):
        present, former, gathered = carry
        padded = with_halo(present, (("gx", 1), ("gy", 2)), 1)
        wavefield = lax.dynamic_index_in_dim(stored, index, 0, keepdims=False)
        advanced = (
            2.0 * present - former + courant_sq * neighbours(padded, present) + gain * wavefield
        )
        live_now = lax.dynamic_index_in_dim(live_mask, index, 1, keepdims=False)
        sampled = jnp.sum(receivers * advanced, axis=3) * live_now[:, None, None]
        gathered = lax.dynamic_update_index_in_dim(gathered, sampled, index, 1)
        return (advanced, present, gathered)

    unused_e, unused_f, records = lax.fori_loop(
        1, step_count, propagate, (first_wave, jnp.zeros_like(first_wave), records)
    )
    partials = (jnp.sum(records * records),)
    partials = partials + (jnp.sum(residual * records), jnp.sum(residual * residual))
    totals = lax.psum(partials, ("shot", "gx", "gy"))
    step_length = slope / totals[0]
    image_next = reflectivity + step_length * direction_next
    residual_next = residual - step_length * records
    entry_count = float(
        shot_count
        * step_count
        * extent_x
        * extent_y
        * lax.axis_size("shot")
        * lax.axis_size("gx")
        * lax.axis_size("gy")
    )
    misfit_sum = totals[2] - 2.0 * step_length * totals[1] + step_length * step_length * totals[0]
    return (image_next, direction_next, residual_next, 0.5 * misfit_sum / entry_count)


def solution(mesh):
    return jax.shard_map(
        on_device,
        mesh=mesh,
        in_specs=(
            P("shot", "gx", "gy", None),
            P("shot", "gx", "gy", None),
            P("gx", "gy", None),
            P("gx", "gy", None),
            P("gx", "gy", None),
            P("gx", "gy", None),
            P("shot", None, "gx", "gy"),
            P("shot", "gx", "gy"),
            P("shot", None),
            P("shot", None),
            P("shot"),
        ),
        out_specs=(P("gx", "gy", None), P("gx", "gy", None), P("shot", None, "gx", "gy"), P()),
        check_vma=False,
    )
```

profile of v0, /device:TPU:0, one launch (start us, length us, event | category | flops | bytes accessed | tf_op | source)
XLA Modules:
  0.0 966.1 jit_solution(17157599112278566666)
XLA Ops:
  13.3 4.3 dynamic_update_slice.32
  17.6 268.8 %while.62 = (s32[]{:T(128)}, f32[1,8,64,256]{3,2,1,0:T(8,128)S(1)}, f32[1,8,64,256]{3,2,1,0:T(8,128)S(1)}, f32[16,1,8,64,256]{4,3,2,1,0:T(8,128)}, f32[8,64,256]...) while((s32[]{:T(128)}, f32[1,8,64,256]{3,2,1,0:T(8,128)S(1)}, ...), condition=%wide.region_1.2_spmd.clone, body=%wide.region_0.1_spmd.clone.sunk | while | flops 2359301 | bytes 7747143 | solution.py:69
  17.6 4.9 collective-permute-start
  24.4 4.2 collective-permute-done.1
  43.3 4.2 collective-permute-done.1
  62.2 4.2 collective-permute-done.1
  81.1 4.2 collective-permute-done.1
  98.5 4.2 collective-permute-done.1
  115.8 4.2 collective-permute-done.1
  150.8 4.2 collective-permute-done.1
  168.4 4.2 collective-permute-done.1
  287.7 258.0 %while.63 = (s32[]{:T(128)}, f32[1,8,64,256]{3,2,1,0:T(8,128)S(1)}, f32[1,8,64,256]{3,2,1,0:T(8,128)S(1)}, f32[1,8,64,256]{3,2,1,0:T(8,128)S(1)}, f32[8,64,256]{...) while((s32[]{:T(128)}, f32[1,8,64,256]{3,2,1,0:T(8,128)S(1)}, ...), condition=%wide.region_3.4_spmd.clone, body=%wide.region_2.3_spmd.clone.sunk | while | flops 3155974 | bytes 9044299 | solution.py:90
  289.2 4.5 collective-permute-start.5
  306.4 4.5 collective-permute-start.5
  323.5 4.5 collective-permute-start.5
  340.7 4.5 collective-permute-start.5
  357.8 4.5 collective-permute-start.5
  375.6 4.5 collective-permute-start.5
  392.7 4.5 collective-permute-start.5
  409.9 4.5 collective-permute-start.5
  427.0 4.5 collective-permute-start.5
  444.2 4.5 collective-permute-start.5
  461.3 4.5 collective-permute-start.5
  478.5 4.5 collective-permute-start.5
  495.6 4.5 collective-permute-start.5
  512.8 4.5 collective-permute-start.5
  529.9 4.5 collective-permute-start.5
  547.1 32.1 %all-reduce.9.cloned.1.call-done = f32[8,64,256]{2,1,0:T(8,128)} async-done(((f32[8,64,256]{2,1,0:T(8,128)}), f32[8,64,256]{2,1,0:T(8,128)}) %all-reduce.9.cloned.1.call-update) | async-done | bytes 524304 | tf_op jit(solution)/shard_map/psum | solution.py:100
  581.1 39.7 %all-reduce.6 = (f32[]{:T(128)}, f32[]{:T(128)}, f32[]{:T(128)}) all-reduce(f32[]{:T(128)} %get-tuple-element.732, f32[]{:T(128)} %get-tuple-element.730, f32[]{:T(128)} %get-tuple-element.731), channel_id=1, replica_groups=mesh['shot'=4,'gx'=2,'gy'=4] {'shot','gx','gy'}, use_global_device_ids=true, to_apply=%region_6.7 | all-reduce | flops 3 | bytes 24 | tf_op jit(solution)/shard_map/psum | solution.py:110
  626.4 286.7 %while.64 = (s32[]{:T(128)}, f32[1,8,64,256]{3,2,1,0:T(8,128)S(1)}, f32[1,8,64,256]{3,2,1,0:T(8,128)S(1)}, f32[1,16,8,64]{3,2,1,0:T(8,128)S(1)}, f32[8,64,256]{2...) while((s32[]{:T(128)}, f32[1,8,64,256]{3,2,1,0:T(8,128)S(1)}, ...), condition=%wide.region_16.17_spmd.clone, body=%wide.region_14.16_spmd.clone.sunk | while | flops 2621445 | bytes 8282455 | solution.py:132
  626.4 4.4 collective-permute-start.8
  913.8 38.0 %all-reduce.5 = (f32[]{:T(128)}, f32[]{:T(128)}, f32[]{:T(128)}, f32[]{:T(128)}) all-reduce(f32[]{:T(128)} %get-tuple-element.729, f32[]{:T(128)} %get-tuple-element.734, f32[]{:T(128)} %get-tuple-element.735, f32[]{:T(128)} %get-tuple-element.733), channel_id=1, replica_groups=mesh['shot'=4,'gx'=2,'gy'=4] {'shot','gx','gy'}, use_global_device_ids=true, to_apply=%region_12.13 | all-reduce | flops 4 | bytes 32 | tf_op jit(solution)/shard_map/psum | solution.py:110
  (763 shorter events, 714.6 us)
Async XLA Ops:
  7.2 572.0 %all-reduce.9.cloned.1.call-start = ((), (), s32[]{:S(2)}) async-start(), calls=%async_computation | async-start | bytes 1048576 | tf_op jit(solution)/shard_map/psum | solution.py:100
  17.6 6.8 collective-permute-start
  22.5 6.2 collective-permute-start.1
  41.4 6.2 collective-permute-start.1
  79.2 6.2 collective-permute-start.1
  96.5 6.2 collective-permute-start.1
  131.2 6.3 collective-permute-start.1
  148.8 6.2 collective-permute-start.1
  166.5 6.2 collective-permute-start.1
  183.9 6.2 collective-permute-start.1
  201.2 6.2 collective-permute-start.1
  218.5 6.2 collective-permute-start.1
  235.9 6.2 collective-permute-start.1
  287.8 6.3 collective-permute-start.4
  289.2 6.4 collective-permute-start.5
  306.4 6.4 collective-permute-start.5
  323.5 6.4 collective-permute-start.5
  340.7 6.4 collective-permute-start.5
  356.5 6.9 collective-permute-start.4
  357.8 6.7 collective-permute-start.5
  375.6 6.4 collective-permute-start.5
  392.7 6.4 collective-permute-start.5
  409.9 6.4 collective-permute-start.5
  427.0 6.4 collective-permute-start.5
  444.2 6.4 collective-permute-start.5
  461.3 6.4 collective-permute-start.5
  478.5 6.4 collective-permute-start.5
  495.6 6.4 collective-permute-start.5
  512.8 6.4 collective-permute-start.5
  529.9 6.4 collective-permute-start.5
  626.4 6.3 collective-permute-start.8
  764.9 6.3 collective-permute-start.9
  (156 other events, 1936.5 us)
Sparse Core Ops, SparseCore 0:
  546.7 32.4 all-reduce.8
where the time goes:
time: 972 us; the launch traced here: 966 us
  waiting for transfers between devices  374 us (38%)
  starting transfers between devices  333 us (34%)
  other arithmetic  106 us (11%)
  blocking collectives  77.7 us (8%)
  local copies, waits for them, and re-layouts  48.7 us (5%)
  between operations  21.7 us (2%)
    ppermute x90, waiting for transfers between devices, with_halo(): after = lax.ppermute(first, axis, down)  300 us
    ppermute x90, starting transfers between devices, with_halo(): before = lax.ppermute(last, axis, up)  217 us
    ppermute x90, starting transfers between devices, with_halo(): after = lax.ppermute(first, axis, down)  116 us
    psum x2, blocking collectives, on_device(): summed = lax.psum(partials, ('shot', 'gx', 'gy'))  77.7 us
    ppermute x90, waiting for transfers between devices, with_halo(): before = lax.ppermute(last, axis, up)  42.3 us
    psum x1, waiting for transfers between devices, on_device(): gradient = lax.psum(local_gradient, 'shot')  32.1 us
    dynamic_update_slice x15, other arithmetic, advance(): history = lax.dynamic_update_index_in_dim(history, advanced, index + 1, 0)  29.5 us
    reduce_sum x15, other arithmetic, propagate(): sampled = jnp.sum(receivers * advanced, axis=3) * live_now[:, None, None]  26.1 us
  transfers between devices with their start and end apart: 181, of which 136 were waited for; matrix products, arithmetic and copies ran while one was open for 3% of the time, Pallas kernels for 0%

commit v1 on v0

v1 whole, which is shorter than its diff:
```python
import functools

import jax
import jax.numpy as jnp
from jax import lax
from jax.experimental import pallas as pl
from jax.experimental.pallas import tpu as pltpu
from jax.sharding import PartitionSpec as P

MESH = pl.DeviceIdType.MESH
LANES = 128


def shifted(v, axis):
    size = v.shape[axis]
    index = lax.broadcasted_iota(jnp.int32, v.shape, axis)
    before = jnp.where(index == 0, 0.0, pltpu.roll(v, 1, axis))
    after = jnp.where(index == size - 1, 0.0, pltpu.roll(v, size - 1, axis))
    return before + after


def advance(below, present, above, former, speed):
    around = (below + above) + shifted(present, 0) + shifted(present, 1)
    return 2.0 * present - former + speed * (around - 6.0 * present)


def fold(v):
    return jnp.sum(v, axis=0, keepdims=True)


def lanes_folded(v):
    total = v[:, :LANES]
    for k in range(1, v.shape[1] // LANES):
        total = total + v[:, k * LANES:(k + 1) * LANES]
    return total


def kernel(
    sizes,
    cell_ref, wave_ref, now_ref, prev_ref, speed_ref, path_ref, old_ref, trace_ref, live_ref, rr_ref,
    dn_out, rec_out, stat_out, total_out,
    both, born, speed, path, old, trace, depth, grad, parts, reduced, gain, dn, dn_home, rec, rec_home,
    tile_a, slots_a, tile_b, slots_b,
    local_sem, home_send, home_recv, edge_send, edge_recv, born_send, born_recv,
    part_send, part_recv, share_send, share_recv, dn_send, dn_recv, rec_send, rec_recv,
    a_send, a_recv, b_send, b_recv,
):
    shots, across, along, steps = sizes
    shot, g, j = lax.axis_index("shot"), lax.axis_index("gx"), lax.axis_index("gy")
    block_y, extent_x, extent_z = now_ref.shape
    rows = block_y // across
    width = extent_x * across

    def snake(column, block):
        return jnp.where(lax.rem(block, 2) == 0, column, across - 1 - column)

    sigma = snake(g, j)
    place = j * across + sigma
    last = across * along - 1

    def chain(position):
        block = lax.div(position, across)
        return {"gx": snake(lax.rem(position, across), block), "gy": block}

    lower = chain(jnp.maximum(place - 1, 0))
    upper = chain(jnp.minimum(place + 1, last))

    targets = (
        (trace_ref, trace),
        (speed_ref, speed),
        (now_ref, both.at[1, pl.ds(1, rows), 0]),
        (prev_ref, both.at[0, pl.ds(1, rows), 0]),
        (path_ref, path),
        (old_ref, old),
    )
    mine = pl.ds(pl.multiple_of(g * extent_x, extent_x), extent_x)
    moves = []
    for k, (source, target) in enumerate(targets):
        own = pltpu.make_async_copy(
            source.at[pl.ds(sigma * rows, rows)], target.at[:, mine], local_sem.at[k]
        )
        own.start()
        group = [own]
        for d in range(1, across):
            peer = lax.rem(g + d, across)
            copy = pltpu.make_async_remote_copy(
                src_ref=source.at[pl.ds(snake(peer, j) * rows, rows)],
                dst_ref=target.at[:, mine],
                send_sem=home_send.at[k, d - 1],
                recv_sem=home_recv.at[k, d - 1],
                device_id={"gx": peer},
                device_id_type=MESH,
            )
            copy.start()
            group.append(copy)
        moves.append(group)

    flat = jnp.zeros((width, extent_z), jnp.float32)

    def clear(r, carry):
        both[0, r + 1, 1] = flat
        born[0, r + 1] = flat
        return carry

    lax.fori_loop(0, rows, clear, 0)
    rec[...] = jnp.zeros(rec.shape, jnp.float32)

    def clear_edge(row):
        def one(n, carry):
            both[n, row, 0] = flat
            both[n, row, 1] = flat
            born[n, row] = flat
            return carry

        lax.fori_loop(1, steps + 1, one, 0)

    @pl.when(place == 0)
    def _():
        clear_edge(0)

    @pl.when(place == last)
    def _():
        clear_edge(rows + 1)

    x_index = lax.broadcasted_iota(jnp.int32, (width, extent_z), 0)
    z_index = lax.broadcasted_iota(jnp.int32, (width, extent_z), 1)
    lane = lax.broadcasted_iota(jnp.int32, (width, LANES), 1)
    z_float = z_index.astype(jnp.float32)
    cell_x, cell_y, cell_z = cell_ref[0, 0], cell_ref[0, 1], cell_ref[0, 2]
    spot = jnp.where((x_index == cell_x) & (z_index == cell_z), 1.0, 0.0)
    first_row = j * block_y + sigma * rows

    def edges(field, n, sends, recvs):
        down = pltpu.make_async_remote_copy(
            src_ref=field.at[n, 1], dst_ref=field.at[n, rows + 1],
            send_sem=sends.at[n, 0], recv_sem=recvs.at[n, 0], device_id=lower, device_id_type=MESH,
        )
        up = pltpu.make_async_remote_copy(
            src_ref=field.at[n, rows], dst_ref=field.at[n, 0],
            send_sem=sends.at[n, 1], recv_sem=recvs.at[n, 1], device_id=upper, device_id_type=MESH,
        )
        return down, up

    def send_edges(field, n, sends, recvs):
        down, up = edges(field, n, sends, recvs)

        @pl.when(place > 0)
        def _():
            down.start()

        @pl.when(place < last)
        def _():
            up.start()

    def wait_edges(field, n, sends, recvs):
        down, up = edges(field, n, sends, recvs)

        @pl.when(place < last)
        def _():
            down.wait_recv()
            up.wait_send()

        @pl.when(place > 0)
        def _():
            up.wait_recv()
            down.wait_send()

    def picked(r, n):
        return jnp.sum(jnp.where(lane == n, trace[r], 0.0), axis=1, keepdims=True)

    def receivers(r):
        level = jnp.concatenate([depth[r]] * (extent_z // LANES), axis=1)
        return level == z_float

    unroll = 1
    for candidate in (2, 3):
        if (rows - 2) % candidate == 0:
            unroll = candidate

    for copy in moves[0]:
        copy.wait()
    for copy in moves[1]:
        copy.wait()

    def adjoint_start(r, carry):
        depth[r] = jnp.broadcast_to(picked(r, steps), (width, LANES))
        weight = picked(r, steps - 1)
        both[1, r + 1, 1] = jnp.where(receivers(r), speed[r] * weight, 0.0)
        return carry

    lax.fori_loop(0, rows, adjoint_start, 0)
    for k in (2, 3):
        for copy in moves[k]:
            copy.wait()
    send_edges(both, 1, edge_send, edge_recv)

    def forward_row(n, r):
        c = speed[r]
        amplitude = jnp.where(first_row + r == cell_y, wave_ref[0, n - 1], 0.0)
        u = advance(both[n, r, 0], both[n, r + 1, 0], both[n, r + 2, 0], both[n - 1, r + 1, 0], c)
        both[n + 1, r + 1, 0] = u + amplitude * spot
        v = advance(both[n, r, 1], both[n, r + 1, 1], both[n, r + 2, 1], both[n - 1, r + 1, 1], c)
        both[n + 1, r + 1, 1] = v + jnp.where(receivers(r), c * picked(r, steps - 1 - n), 0.0)

    def sweep(row_of, n):
        def one(r, carry):
            row_of(n, r)
            return carry

        lax.fori_loop(1, rows - 1, one, 0, unroll=unroll)

    def forward(n, carry):
        sweep(forward_row, n)
        wait_edges(both, n, edge_send, edge_recv)
        forward_row(n, 0)
        forward_row(n, rows - 1)

        @pl.when(n < steps - 1)
        def _():
            send_edges(both, n + 1, edge_send, edge_recv)

        return carry

    lax.fori_loop(1, steps, forward, 0)

    def image_row(r, carry):
        total = both[1, r + 1, 0] * both[steps, r + 1, 1]
        for a in range(2, steps + 1):
            total = total + both[a, r + 1, 0] * both[steps + 1 - a, r + 1, 1]
        grad[r] = total
        return carry

    lax.fori_loop(0, rows, image_row, 0)
    share = rows // shots
    copies = []
    for d in range(1, shots):
        peer = lax.rem(shot + d, shots)
        copy = pltpu.make_async_remote_copy(
            src_ref=grad.at[pl.ds(peer * share, share)], dst_ref=parts.at[d - 1],
            send_sem=part_send.at[d - 1], recv_sem=part_recv.at[d - 1],
            device_id={"shot": peer}, device_id_type=MESH,
        )
        copy.start()
        copies.append(copy)
    for copy in copies:
        copy.wait()
    own_share = shot * share

    def add_share(r, carry):
        total = grad[own_share + r]
        for d in range(1, shots):
            total = total + parts[d - 1, r]
        reduced[own_share + r] = total
        return carry

    lax.fori_loop(0, share, add_share, 0)
    copies = []
    for d in range(1, shots):
        peer = lax.rem(shot + d, shots)
        copy = pltpu.make_async_remote_copy(
            src_ref=reduced.at[pl.ds(own_share, share)], dst_ref=reduced.at[pl.ds(own_share, share)],
            send_sem=share_send.at[d - 1], recv_sem=share_recv.at[d - 1],
            device_id={"shot": peer}, device_id_type=MESH,
        )
        copy.start()
        copies.append(copy)
    for k in (4, 5):
        for copy in moves[k]:
            copy.wait()
    for copy in copies:
        copy.wait()

    zero = jnp.zeros((width, LANES), jnp.float32)

    def inner(r, carry):
        new, was, way = reduced[r], old[r], path[r]
        return (
            carry[0] + lanes_folded(new * new),
            carry[1] + lanes_folded(new * was),
            carry[2] + lanes_folded(was * was),
            carry[3] + lanes_folded(new * way),
        )

    sums = lax.fori_loop(0, rows, inner, (zero, zero, zero, zero))

    def write_tile(tile, values):
        tile[...] = jnp.concatenate(
            [fold(v) for v in values] + [jnp.zeros((8 - len(values), LANES), jnp.float32)], axis=0
        )

    def all_sum(tile, slots, count, rank, device_of, sends, recvs):
        copies = []
        for d in range(1, count):
            copy = pltpu.make_async_remote_copy(
                src_ref=tile, dst_ref=slots.at[rank],
                send_sem=sends.at[d - 1], recv_sem=recvs.at[d - 1],
                device_id=device_of(lax.rem(rank + d, count)), device_id_type=MESH,
            )
            copy.start()
            copies.append(copy)
        slots[rank] = tile[...]
        for copy in copies:
            copy.wait()
        return lax.fori_loop(0, count, lambda k, total: total + slots[k], jnp.zeros((8, LANES), jnp.float32))

    grid_rank = g * along + j
    write_tile(tile_a, sums)
    stats = all_sum(
        tile_a, slots_a, across * along, grid_rank,
        lambda k: {"gx": lax.div(k, along), "gy": lax.rem(k, along)}, a_send, a_recv,
    )
    stat_out[...] = stats
    values = jnp.sum(stats, axis=1, keepdims=True)
    beta = (values[0:1] - values[1:2]) / values[2:3]

    def search(r, carry):
        new = reduced[r] + beta * path[r]
        dn[r] = new
        lift = speed[r] * new
        gain[r] = lift
        born[1, r + 1] = lift * both[1, r + 1, 0]
        return carry

    lax.fori_loop(0, rows, search, 0)
    send_edges(born, 1, born_send, born_recv)

    def homeward(field, home, sends, recvs):
        strip = pl.ds(sigma * rows, rows)
        copies = []
        for d in range(1, across):
            peer = lax.rem(g + d, across)
            part = pl.ds(pl.multiple_of(peer * extent_x, extent_x), extent_x)
            copies.append(pltpu.make_async_remote_copy(
                src_ref=field.at[:, part], dst_ref=home.at[strip],
                send_sem=sends.at[d], recv_sem=recvs.at[d - 1],
                device_id={"gx": peer}, device_id_type=MESH,
            ))
        copies.append(pltpu.make_async_copy(field.at[:, mine], home.at[strip], sends.at[0]))
        for copy in copies:
            copy.start()
        return copies

    def sample(n, r, w):
        hit = jnp.sum(jnp.where(receivers(r), w, 0.0), axis=1, keepdims=True)
        rec[r] = jnp.where(lane == n - 1, hit, rec[r])

    def first_sample(r, carry):
        sample(1, r, born[1, r + 1])
        return carry

    lax.fori_loop(0, rows, first_sample, 0)

    def born_row(n, r):
        w = advance(born[n, r], born[n, r + 1], born[n, r + 2], born[n - 1, r + 1], speed[r])
        w = w + gain[r] * both[n + 1, r + 1, 0]
        born[n + 1, r + 1] = w
        sample(n + 1, r, w)

    def scatter(n, carry):
        sweep(born_row, n)
        wait_edges(born, n, born_send, born_recv)
        born_row(n, 0)
        born_row(n, rows - 1)

        @pl.when(n < steps - 1)
        def _():
            send_edges(born, n + 1, born_send, born_recv)

        return carry

    lax.fori_loop(1, steps, scatter, 0)
    dn_moves = homeward(dn, dn_home, dn_send, dn_recv)

    def finish(r, carry):
        row = rec[r] * live_ref[0:1]
        rec[r] = row
        return carry[0] + row * row, carry[1] + trace[r] * row

    sums = lax.fori_loop(0, rows, finish, (zero, zero))
    write_tile(tile_b, sums + (rr_ref[...],))
    rec_moves = homeward(rec, rec_home, rec_send, rec_recv)
    grid = across * along
    total_out[...] = all_sum(
        tile_b, slots_b, shots * grid, shot * grid + grid_rank,
        lambda k: {
            "shot": lax.div(k, grid),
            "gx": lax.div(lax.rem(k, grid), along),
            "gy": lax.rem(k, along),
        },
        b_send, b_recv,
    )
    for copy in dn_moves + rec_moves:
        copy.wait()
    dn_out[...] = dn_home[...]
    rec_out[...] = rec_home[...]


def on_device(
    state_now, state_prev, courant_sq, reflectivity, direction, prev_gradient,
    residual, rec_depth, source_cell, wavelet, live_steps,
):
    shots, across, along = (lax.axis_size(a) for a in ("shot", "gx", "gy"))
    steps = residual.shape[1]
    extent_x, block_y, extent_z = courant_sq.shape
    rows, width = block_y // across, extent_x * across

    def turned(v):
        return jnp.transpose(v, (1, 0, 2))

    live = (lax.iota(jnp.int32, steps) < live_steps[0]).astype(jnp.float32)
    weighted = residual[0] * live[:, None, None]
    packed = jnp.concatenate([weighted, rec_depth.astype(jnp.float32)], axis=0)
    packed = jnp.pad(jnp.transpose(packed, (2, 1, 0)), ((0, 0), (0, 0), (0, LANES - steps - 1)))
    live_lanes = jnp.broadcast_to(jnp.pad(live, (0, LANES - steps)), (8, LANES))
    squares = jnp.sum(residual * residual)
    rr = jnp.pad(squares.reshape(1, 1), ((0, 7), (0, LANES - 1)))

    f32 = jnp.float32
    strip = (rows, width, extent_z)
    home = (block_y, extent_x, extent_z)
    grid = across * along
    dma = pltpu.SemaphoreType.DMA
    one = max(across - 1, 1)
    scratch = [
        pltpu.VMEM((steps + 1, rows + 2, 2, width, extent_z), f32),
        pltpu.VMEM((steps + 1, rows + 2, width, extent_z), f32),
        pltpu.VMEM(strip, f32),
        pltpu.VMEM(strip, f32),
        pltpu.VMEM(strip, f32),
        pltpu.VMEM((rows, width, LANES), f32),
        pltpu.VMEM((rows, width, LANES), f32),
        pltpu.VMEM(strip, f32),
        pltpu.VMEM((shots - 1, rows // shots, width, extent_z), f32),
        pltpu.VMEM(strip, f32),
        pltpu.VMEM(strip, f32),
        pltpu.VMEM(strip, f32),
        pltpu.VMEM(home, f32),
        pltpu.VMEM((rows, width, LANES), f32),
        pltpu.VMEM((block_y, extent_x, LANES), f32),
        pltpu.VMEM((8, LANES), f32),
        pltpu.VMEM((grid, 8, LANES), f32),
        pltpu.VMEM((8, LANES), f32),
        pltpu.VMEM((shots * grid, 8, LANES), f32),
        dma((6,)), dma((6, one)), dma((6, one)),
        dma((steps + 1, 2)), dma((steps + 1, 2)), dma((steps + 1, 2)), dma((steps + 1, 2)),
        dma((shots - 1,)), dma((shots - 1,)), dma((shots - 1,)), dma((shots - 1,)),
        dma((across,)), dma((one,)), dma((across,)), dma((one,)),
        dma((grid - 1,)), dma((grid - 1,)), dma((shots * grid - 1,)), dma((shots * grid - 1,)),
    ]
    vmem, smem = pl.BlockSpec(memory_space=pltpu.VMEM), pl.BlockSpec(memory_space=pltpu.SMEM)
    dn, rec, stats, totals = pl.pallas_call(
        functools.partial(kernel, (shots, across, along, steps)),
        out_shape=(
            jax.ShapeDtypeStruct(home, f32),
            jax.ShapeDtypeStruct((block_y, extent_x, LANES), f32),
            jax.ShapeDtypeStruct((8, LANES), f32),
            jax.ShapeDtypeStruct((8, LANES), f32),
        ),
        in_specs=[smem, smem] + [vmem] * 8,
        out_specs=(vmem,) * 4,
        scratch_shapes=scratch,
        compiler_params=pltpu.CompilerParams(has_side_effects=True, vmem_limit_bytes=60 * 1024 * 1024),
        name="iteration",
    )(
        source_cell, wavelet, turned(state_now[0]), turned(state_prev[0]), turned(courant_sq),
        turned(direction), turned(prev_gradient), packed, live_lanes, rr,
    )
    sums = jnp.sum(stats, axis=1)
    ends = jnp.sum(totals, axis=1)
    beta = (sums[0] - sums[1]) / sums[2]
    slope = sums[0] + beta * sums[3]
    step = slope / ends[0]
    direction_next = turned(dn)
    image_next = reflectivity + step * direction_next
    records = jnp.transpose(rec[:, :, :steps], (2, 1, 0))
    residual_next = residual - step * records[None]
    entries = float(residual.size * shots * grid)
    misfit = ends[2] - 2.0 * step * ends[1] + step * step * ends[0]
    return image_next, direction_next, residual_next, 0.5 * misfit / entries


def solution(mesh):
    field, flat = P("shot", "gx", "gy", None), P("gx", "gy", None)
    traces = P("shot", None, "gx", "gy")
    return jax.shard_map(
        on_device,
        mesh=mesh,
        in_specs=(
            field, field, flat, flat, flat, flat, traces,
            P("shot", "gx", "gy"), P("shot", None), P("shot", None), P("shot"),
        ),
        out_specs=(flat, flat, traces, P()),
        check_vma=False,
    )
```

time: 972 us -> 187 us (0.19)
  waiting for transfers between devices: 374 us -> 0 us
  starting transfers between devices: 333 us -> 0 us
  Pallas kernels: 0 us -> 162 us
  other arithmetic: 106 us -> 2.69 us
  blocking collectives: 77.7 us -> 0 us
  local copies, waits for them, and re-layouts: 48.7 us -> 13.3 us
  between operations: 21.7 us -> 8.46 us
    ppermute x180 -> x0, waiting for transfers between devices: 342 us -> none  [the longest x90 300 us: with_halo(): after = lax.ppermute(first, axis, down)]
    ppermute x180 -> x0, starting transfers between devices: 333 us -> none  [the longest x90 217 us: with_halo(): before = lax.ppermute(last, axis, up)]
    pallas_call x0 -> x1, Pallas kernels: none -> 162 us  [on_device(): pl.pallas_call(functools.partial(kernel, (shots, across, along, steps)),...]
    psum x2 -> x0, blocking collectives: 77.7 us -> none  [on_device(): summed = lax.psum(partials, ('shot', 'gx', 'gy'))]
    dynamic_update_slice x30 -> x0, other arithmetic: 39.1 us -> none  [the longest x15 29.5 us: advance(): history = lax.dynamic_update_index_in_dim(history, advanced, index + 1, 0)]
    psum x1 -> x0, waiting for transfers between devices: 32.1 us -> none  [on_device(): gradient = lax.psum(local_gradient, 'shot')]
    reduce_sum x18 -> x3, other arithmetic: 30.3 us -> 2.25 us  [the longest x1 0.84 us: on_device(): sums = jnp.sum(stats, axis=1)]
    dynamic_slice x30 -> x0, local copies, waits for them, and re-layouts: 27.1 us -> none  [the longest x15 18.3 us: propagate(): live_now = lax.dynamic_index_in_dim(live_mask, index, 1, keepdims=False)]
  transfers between devices with their start and end apart: 181 -> 0, of which waited for: 136 -> 0; matrix products, arithmetic and copies ran while one was open for 3% -> 0% of each run, Pallas kernels for 0% -> 0%
where the time goes in v1:
time: 187 us
  Pallas kernels  162 us (87%)
  local copies, waits for them, and re-layouts  13.3 us (7%)
  between operations  8.46 us (5%)
  other arithmetic  2.69 us (1%)
    pallas_call x1, Pallas kernels, on_device(): pl.pallas_call(functools.partial(kernel, (shots, across, along, steps)),...  162 us
    unnamed x21, local copies, waits for them, and re-layouts  4.96 us
    transpose x2, local copies, waits for them, and re-layouts, turned(): return jnp.transpose(v, (1, 0, 2))  4.45 us

profile of v1, /device:TPU:0, one launch (start us, length us, event | category | flops | bytes accessed | tf_op | source)
XLA Modules:
  0.0 186.6 jit_solution(14811900833118005387)
XLA Ops:
  0.6 0.0 copy-start.5
  0.6 0.0 copy-start.4
  0.7 2.9 %copy_bitcast_fusion = (f32[64,8,256]{2,1,0:T(8,128)}, f32[64,8,256]{2,1,0:T(8,128)}) fusion(f32[8,64,256]{2,1,0:T(8,128)} %param.16, f32[8,64,256]{2,1,0:T(8,128)} %param.15), kind=kLoop, calls=%fused_computation.1 | loop fusion | bytes 2097152 | tf_op jit(solution)/shard_map/transpose | solution.py:408
  3.5 0.0 copy-done.5
  3.5 0.0 copy-done.4
  3.5 1.6 copy_bitcast_fusion.3
  5.8 0.0 copy-done.1
  5.8 0.0 copy-start.7
  5.8 0.1 bitcast_multiply_fusion
  5.9 0.6 copy-done.7
  6.5 0.2 copy.32
  6.7 0.7 pad.12.trace_ref
  7.4 0.6 broadcast_in_dim.2.live_ref
  8.0 0.0 copy-done.2
  8.0 1.1 copy.44
  9.1 0.6 multiply_reduce_fusion
  9.7 1.2 pad.14.rr_ref
  11.0 162.1 %iteration.1 = (f32[64,8,256]{2,1,0:T(8,128)}, f32[64,8,128]{2,1,0:T(8,128)}, f32[8,128]{1,0:T(8,128)}, f32[8,128]{1,0:T(8,128)}) custom-call(s32[1,3]{1,0:T(1,128)} %cell_ref.1, f32[1,15]{1,0:T(1,128)} %wave_ref.1, f32[64,8,256]{2,1,0:T(8,128)} %get-tuple-element.30.now_ref, f32[64,8,256]{2,1,0:T(8,128)} %get-tuple-element.29.prev_ref, ...), custom_call_target="tpu_custom_call" | custom-call | tf_op jit(solution)/shard_map/iteration/pallas_call | solution.py:451
  173.1 0.8 reduce_sum.28
  174.0 0.6 fusion.1
  177.8 0.8 reduce_sum.29
  178.6 0.6 fusion
  181.9 0.2 copy.34
  182.0 0.0 copy-done.6
  182.0 0.0 copy-start
  182.1 0.0 copy-start.3
  182.1 0.8 copy.37
  182.9 0.2 copy-done
  183.1 0.2 copy-done.3
  183.3 0.3 copy_add_fusion
  183.6 1.0 copy.35
  184.5 1.0 copy.36
  (8 shorter events, 0.1 us)
Async XLA Ops:
  0.6 2.9 %copy-start.5 = (f32[1,8,64,256]{3,2,1,0:T(8,128)S(1)}, f32[1,8,64,256]{3,2,1,0:T(8,128)}, u32[]{:S(2)}) copy-start(f32[1,8,64,256]{3,2,1,0:T(8,128)} %param.11) | copy-start | bytes 1572868
  0.6 2.9 %copy-start.4 = (f32[1,8,64,256]{3,2,1,0:T(8,128)S(1)}, f32[1,8,64,256]{3,2,1,0:T(8,128)}, u32[]{:S(2)}) copy-start(f32[1,8,64,256]{3,2,1,0:T(8,128)} %param.12) | copy-start | bytes 1572868
  3.5 2.2 %copy-start.1 = (f32[1,16,8,64]{3,2,1,0:T(8,128)S(1)}, f32[1,16,8,64]{3,2,1,0:T(8,128)}, u32[]{:S(2)}) copy-start(f32[1,16,8,64]{3,2,1,0:T(8,128)} %param.17) | copy-start | bytes 98308
  5.8 0.7 copy-start.7
  6.5 1.5 copy-start.2
  173.1 8.9 %copy-start.6 = (f32[64,8,128]{2,1,0:T(8,128)S(1)}, f32[64,8,128]{2,1,0:T(8,128)}, u32[]{:S(2)}) copy-start(f32[64,8,128]{2,1,0:T(8,128)} %get-tuple-element.11) | copy-start | bytes 786436
  182.0 1.0 copy-start
  182.1 1.2 copy-start.3

commit v2 on v1

v2 whole, which is shorter than its diff:
```python
import functools

import jax
import jax.numpy as jnp
from jax import lax
from jax.experimental import pallas as pl
from jax.experimental.pallas import tpu as pltpu
from jax.sharding import PartitionSpec as P

MESH = pl.DeviceIdType.MESH
LANES = 128


def shifted(v, axis):
    size = v.shape[axis]
    index = lax.broadcasted_iota(jnp.int32, v.shape, axis)
    before = jnp.where(index == 0, 0.0, pltpu.roll(v, 1, axis))
    after = jnp.where(index == size - 1, 0.0, pltpu.roll(v, size - 1, axis))
    return before + after


def advance(below, present, above, former, speed):
    around = (below + above) + shifted(present, 0) + shifted(present, 1)
    return 2.0 * present - former + speed * (around - 6.0 * present)


def fold(v):
    return jnp.sum(v, axis=0, keepdims=True)


def lanes_folded(v):
    total = v[:, :LANES]
    for k in range(1, v.shape[1] // LANES):
        total = total + v[:, k * LANES:(k + 1) * LANES]
    return total


def kernel(
    sizes,
    cell_ref, wave_ref, now_ref, prev_ref, speed_ref, path_ref, old_ref, trace_ref, live_ref, rr_ref,
    dn_out, rec_out, stat_out, total_out,
    both, born, speed, path, old, trace, depth, grad, parts, reduced, gain, dn, dn_home, rec, rec_home,
    tile_a, slots_a, tile_b, slots_b,
    local_sem, home_send, home_recv, later_send, later_recv, edge_send, edge_recv, born_send, born_recv, once_send, once_recv,
    part_send, part_recv, share_send, share_recv, dn_send, dn_recv, rec_send, rec_recv,
    a_send, a_recv, b_send, b_recv,
):
    shots, across, along, steps, fit, chunks = sizes
    shot, g, j = lax.axis_index("shot"), lax.axis_index("gx"), lax.axis_index("gy")
    block_y, extent_x, extent_z = now_ref.shape
    rows = block_y // across
    width = extent_x * across
    size = rows // chunks

    def snake(column, block):
        return jnp.where(lax.rem(block, 2) == 0, column, across - 1 - column)

    sigma = snake(g, j)
    place = j * across + sigma
    last = across * along - 1

    def chain(position):
        block = lax.div(position, across)
        return {"gx": snake(lax.rem(position, across), block), "gy": block}

    lower = chain(jnp.maximum(place - 1, 0))
    upper = chain(jnp.minimum(place + 1, last))

    targets = (
        (trace_ref, trace.at[pl.ds(1, rows // fit)]),
        (speed_ref, speed.at[pl.ds(1, rows)]),
        (now_ref, both.at[1, pl.ds(2, rows), 0]),
        (prev_ref, both.at[0, pl.ds(2, rows), 0]),
    )
    later = ((path_ref, path), (old_ref, old))
    mine = pl.ds(pl.multiple_of(g * extent_x, extent_x), extent_x)
    moves = []
    for k, (source, target) in enumerate(targets):
        count = target.shape[0]
        own = pltpu.make_async_copy(
            source.at[pl.ds(sigma * count, count)], target.at[:, mine], local_sem.at[k]
        )
        own.start()
        group = [own]
        for d in range(1, across):
            peer = lax.rem(g + d, across)
            copy = pltpu.make_async_remote_copy(
                src_ref=source.at[pl.ds(snake(peer, j) * count, count)],
                dst_ref=target.at[:, mine],
                send_sem=home_send.at[k, d - 1],
                recv_sem=home_recv.at[k, d - 1],
                device_id={"gx": peer},
                device_id_type=MESH,
            )
            copy.start()
            group.append(copy)
        moves.append(group)
    own_later = []
    for k, (source, target) in enumerate(later):
        own = pltpu.make_async_copy(
            source.at[pl.ds(sigma * rows, rows)], target.at[:, mine], local_sem.at[len(targets) + k]
        )
        own.start()
        own_later.append(own)

    def later_copies(k, e):
        source, target = later[k]
        copies = []
        for d in range(1, across):
            peer = lax.rem(g + d, across)
            copies.append(pltpu.make_async_remote_copy(
                src_ref=source.at[pl.ds(snake(peer, j) * rows + e * size, size)],
                dst_ref=target.at[pl.ds(e * size, size), mine],
                send_sem=later_send.at[k, d - 1, e], recv_sem=later_recv.at[k, d - 1, e],
                device_id={"gx": peer}, device_id_type=MESH,
            ))
        return copies

    flat = jnp.zeros((width, extent_z), jnp.float32)

    def clear(r, carry):
        both[0, r, 1] = flat
        born[0, r] = flat
        return carry

    lax.fori_loop(0, rows + 4, clear, 0)
    rec[...] = jnp.zeros(rec.shape, jnp.float32)

    def clear_edge(first, single, line):
        def one(n, carry):
            for row in (first, first + 1):
                both[n, row, 0] = flat
                both[n, row, 1] = flat
                born[n, row] = flat
            return carry

        lax.fori_loop(0, steps + 1, one, 0)
        speed[single] = flat
        gain[single] = flat
        trace[line] = flat[:, :LANES]

    @pl.when(place == 0)
    def _():
        clear_edge(0, 0, 0)

    @pl.when(place == last)
    def _():
        clear_edge(rows + 2, rows + 1, rows // fit + 1)

    x_index = lax.broadcasted_iota(jnp.int32, (width, extent_z), 0)
    z_index = lax.broadcasted_iota(jnp.int32, (width, extent_z), 1)
    lane = lax.broadcasted_iota(jnp.int32, (width, LANES), 1)
    z_float = z_index.astype(jnp.float32)
    cell_x, cell_y, cell_z = cell_ref[0, 0], cell_ref[0, 1], cell_ref[0, 2]
    spot = jnp.where((x_index == cell_x) & (z_index == cell_z), 1.0, 0.0)
    first_row = j * block_y + sigma * rows

    def pair(view, own, pad, deep, sends, recvs, k):
        down = pltpu.make_async_remote_copy(
            src_ref=view(pad, deep), dst_ref=view(pad + own, deep),
            send_sem=sends.at[k, 0], recv_sem=recvs.at[k, 0], device_id=lower, device_id_type=MESH,
        )
        up = pltpu.make_async_remote_copy(
            src_ref=view(pad + own - deep, deep), dst_ref=view(pad - deep, deep),
            send_sem=sends.at[k, 1], recv_sem=recvs.at[k, 1], device_id=upper, device_id_type=MESH,
        )
        return down, up

    def both_edges(n):
        return pair(lambda a, c: both.at[n, pl.ds(a, c)], rows, 2, 2, edge_send, edge_recv, n)

    def born_edges(n):
        return pair(lambda a, c: born.at[n, pl.ds(a, c)], rows, 2, 2, born_send, born_recv, n)

    def once_edges(k):
        if k == 0:
            return pair(lambda a, c: trace.at[pl.ds(a, c)], rows // fit, 1, 1, once_send, once_recv, k)
        if k == 2:
            return pair(lambda a, c: both.at[0, pl.ds(a, c), 0], rows, 2, 1, once_send, once_recv, k)
        field = speed if k == 1 else gain
        return pair(lambda a, c: field.at[pl.ds(a, c)], rows, 1, 1, once_send, once_recv, k)

    def send_edges(copies):
        @pl.when(place > 0)
        def _():
            copies[0].start()

        @pl.when(place < last)
        def _():
            copies[1].start()

    def wait_edges(copies):
        @pl.when(place < last)
        def _():
            copies[0].wait_recv()
            copies[1].wait_send()

        @pl.when(place > 0)
        def _():
            copies[1].wait_recv()
            copies[0].wait_send()

    def place_of(r, n):
        line = r // fit if isinstance(r, int) else lax.div(r, fit)
        return line, lane == (r - line * fit) * (LANES // fit) + n

    def picked(r, n):
        line, chosen = place_of(r + fit, n)
        return jnp.sum(jnp.where(chosen, trace[line], 0.0), axis=1, keepdims=True)

    def receivers(r):
        level = jnp.concatenate([depth[r + 1]] * (extent_z // LANES), axis=1)
        return level == z_float

    def inside(r, v):
        if isinstance(r, int) and r < 0:
            return jnp.where(place > 0, v, 0.0)
        if isinstance(r, int) and r >= rows:
            return jnp.where(place < last, v, 0.0)
        return v

    def together(ops, n, where):
        values = [ops[0](n, r) for r in where]
        for r, value in zip(where, values):
            ops[1](n, r, value)

    def sweep(ops, n, first, count):
        group = 1
        for candidate in (2, 3):
            if count % candidate == 0:
                group = candidate

        def one(i, carry):
            together(ops, n, [first + i * group + k for k in range(group)])
            return carry

        lax.fori_loop(0, count // group, one, 0)

    rounds = (steps - 1) // 2

    def march(ops, edges_of, before_edges, after_send):
        def step_pair(i, carry):
            n = 1 + 2 * i
            sweep(ops, n, 1, rows - 2)
            sweep(ops, n + 1, 2, rows - 4)
            wait_edges(edges_of(n))

            @pl.when(i == 0)
            def _():
                before_edges()

            together(ops, n, [-1, 0, rows - 1, rows])
            together(ops, n + 1, [0, 1, rows - 2, rows - 1])

            @pl.when(n + 2 < steps)
            def _():
                send_edges(edges_of(n + 2))

            after_send(i)
            return carry

        lax.fori_loop(0, rounds, step_pair, 0)
        if (steps - 1) % 2:
            sweep(ops, steps - 1, 1, rows - 2)
            wait_edges(edges_of(steps - 1))
            together(ops, steps - 1, [0, rows - 1])

    for copy in moves[0]:
        copy.wait()
    for copy in moves[1]:
        copy.wait()

    for k in (0, 1):
        send_edges(once_edges(k))

    def adjoint_start(r, carry):
        depth[r + 1] = jnp.broadcast_to(picked(r, steps), (width, LANES))
        weight = picked(r, steps - 1)
        both[1, r + 2, 1] = jnp.where(receivers(r), speed[r + 1] * weight, 0.0)
        return carry

    lax.fori_loop(0, rows, adjoint_start, 0)
    for k in (2, 3):
        for copy in moves[k]:
            copy.wait()
    send_edges(both_edges(1))
    send_edges(once_edges(2))

    def forward_value(n, r):
        c = speed[r + 1]
        amplitude = jnp.where(first_row + r == cell_y, wave_ref[0, n - 1], 0.0)
        u = advance(both[n, r + 1, 0], both[n, r + 2, 0], both[n, r + 3, 0], both[n - 1, r + 2, 0], c)
        v = advance(both[n, r + 1, 1], both[n, r + 2, 1], both[n, r + 3, 1], both[n - 1, r + 2, 1], c)
        v = v + jnp.where(receivers(r), c * picked(r, steps - 1 - n), 0.0)
        return inside(r, u + amplitude * spot), inside(r, v)

    def forward_put(n, r, value):
        both[n + 1, r + 2, 0], both[n + 1, r + 2, 1] = value

    def first_halos():
        for k in (0, 1, 2):
            wait_edges(once_edges(k))
        for r in (-1, rows):
            depth[r + 1] = jnp.broadcast_to(picked(r, steps), (width, LANES))

    def regroup_later(i):
        for k, offset in ((0, 0), (1, rounds - chunks)):
            @pl.when((i >= offset) & (i < offset + chunks))
            def _():
                for copy in later_copies(k, i - offset):
                    copy.start()

    march((forward_value, forward_put), both_edges, first_halos, regroup_later)

    def image_row(r, carry):
        total = both[1, r + 2, 0] * both[steps, r + 2, 1]
        for a in range(2, steps + 1):
            total = total + both[a, r + 2, 0] * both[steps + 1 - a, r + 2, 1]
        grad[r] = total
        return carry

    lax.fori_loop(0, rows, image_row, 0)
    share = rows // shots
    copies = []
    for d in range(1, shots):
        peer = lax.rem(shot + d, shots)
        copy = pltpu.make_async_remote_copy(
            src_ref=grad.at[pl.ds(peer * share, share)], dst_ref=parts.at[d - 1],
            send_sem=part_send.at[d - 1], recv_sem=part_recv.at[d - 1],
            device_id={"shot": peer}, device_id_type=MESH,
        )
        copy.start()
        copies.append(copy)
    for copy in copies:
        copy.wait()
    own_share = shot * share

    def add_share(r, carry):
        total = grad[own_share + r]
        for d in range(1, shots):
            total = total + parts[d - 1, r]
        reduced[own_share + r] = total
        return carry

    lax.fori_loop(0, share, add_share, 0)
    copies = []
    for d in range(1, shots):
        peer = lax.rem(shot + d, shots)
        copy = pltpu.make_async_remote_copy(
            src_ref=reduced.at[pl.ds(own_share, share)], dst_ref=reduced.at[pl.ds(own_share, share)],
            send_sem=share_send.at[d - 1], recv_sem=share_recv.at[d - 1],
            device_id={"shot": peer}, device_id_type=MESH,
        )
        copy.start()
        copies.append(copy)
    for copy in own_later:
        copy.wait()

    def later_wait(e, carry):
        for copy in later_copies(0, e) + later_copies(1, e):
            copy.wait()
        return carry

    lax.fori_loop(0, chunks, later_wait, 0)
    for copy in copies:
        copy.wait()

    zero = jnp.zeros((width, LANES), jnp.float32)

    def inner(r, carry):
        new, was, way = reduced[r], old[r], path[r]
        return (
            carry[0] + lanes_folded(new * new),
            carry[1] + lanes_folded(new * was),
            carry[2] + lanes_folded(was * was),
            carry[3] + lanes_folded(new * way),
        )

    sums = lax.fori_loop(0, rows, inner, (zero, zero, zero, zero))

    def write_tile(tile, values):
        tile[...] = jnp.concatenate(
            [fold(v) for v in values] + [jnp.zeros((8 - len(values), LANES), jnp.float32)], axis=0
        )

    def all_sum(tile, slots, count, rank, device_of, sends, recvs):
        copies = []
        for d in range(1, count):
            copy = pltpu.make_async_remote_copy(
                src_ref=tile, dst_ref=slots.at[rank],
                send_sem=sends.at[d - 1], recv_sem=recvs.at[d - 1],
                device_id=device_of(lax.rem(rank + d, count)), device_id_type=MESH,
            )
            copy.start()
            copies.append(copy)
        slots[rank] = tile[...]
        for copy in copies:
            copy.wait()
        return lax.fori_loop(0, count, lambda k, total: total + slots[k], jnp.zeros((8, LANES), jnp.float32))

    grid_rank = g * along + j
    write_tile(tile_a, sums)
    stats = all_sum(
        tile_a, slots_a, across * along, grid_rank,
        lambda k: {"gx": lax.div(k, along), "gy": lax.rem(k, along)}, a_send, a_recv,
    )
    stat_out[...] = stats
    values = jnp.sum(stats, axis=1, keepdims=True)
    beta = (values[0:1] - values[1:2]) / values[2:3]

    def search(r, carry):
        new = reduced[r] + beta * path[r]
        dn[r] = new
        lift = speed[r + 1] * new
        gain[r + 1] = lift
        born[1, r + 2] = lift * both[1, r + 2, 0]
        return carry

    lax.fori_loop(0, rows, search, 0)
    send_edges(once_edges(3))
    send_edges(born_edges(1))

    def homeward(field, home, first, count, send_of, recv_of):
        copies = []
        for d in range(1, across):
            peer = lax.rem(g + d, across)
            part = pl.ds(pl.multiple_of(peer * extent_x, extent_x), extent_x)
            copies.append(pltpu.make_async_remote_copy(
                src_ref=field.at[pl.ds(first, count), part],
                dst_ref=home.at[pl.ds(sigma * field.shape[0] + first, count)],
                send_sem=send_of(d), recv_sem=recv_of(d - 1),
                device_id={"gx": peer}, device_id_type=MESH,
            ))
        copies.append(pltpu.make_async_copy(
            field.at[pl.ds(first, count), mine],
            home.at[pl.ds(sigma * field.shape[0] + first, count)], send_of(0),
        ))
        return copies

    def dn_copies(e):
        return homeward(
            dn, dn_home, e * size, size, lambda d: dn_send.at[d, e], lambda d: dn_recv.at[d, e]
        )

    def hit_of(r, w):
        return jnp.sum(jnp.where(receivers(r), w, 0.0), axis=1, keepdims=True)

    def sample(n, r, hit):
        line, chosen = place_of(r, n - 1)
        rec[line] = jnp.where(chosen, hit, rec[line])

    def first_sample(r, carry):
        sample(1, r, hit_of(r, born[1, r + 2]))
        return carry

    lax.fori_loop(0, rows, first_sample, 0)

    def born_value(n, r):
        w = advance(born[n, r + 1], born[n, r + 2], born[n, r + 3], born[n - 1, r + 2], speed[r + 1])
        w = inside(r, w + gain[r + 1] * both[n + 1, r + 2, 0])
        if isinstance(r, int) and not 0 <= r < rows:
            return w, None
        return w, hit_of(r, w)

    def born_put(n, r, value):
        born[n + 1, r + 2] = value[0]
        if value[1] is not None:
            sample(n + 1, r, value[1])

    def return_dn(i):
        @pl.when(i < chunks)
        def _():
            for copy in dn_copies(i):
                copy.start()

    march((born_value, born_put), born_edges, lambda: wait_edges(once_edges(3)), return_dn)

    def finish(r, carry):
        row = rec[r] * live_ref[0:1]
        rec[r] = row
        return carry[0] + row * row, carry[1] + trace[r + 1] * row

    sums = lax.fori_loop(0, rows // fit, finish, (zero, zero))
    write_tile(tile_b, sums + (rr_ref[...],))
    rec_moves = homeward(
        rec, rec_home, 0, rows // fit, lambda d: rec_send.at[d], lambda d: rec_recv.at[d]
    )
    for copy in rec_moves:
        copy.start()
    grid = across * along
    total_out[...] = all_sum(
        tile_b, slots_b, shots * grid, shot * grid + grid_rank,
        lambda k: {
            "shot": lax.div(k, grid),
            "gx": lax.div(lax.rem(k, grid), along),
            "gy": lax.rem(k, along),
        },
        b_send, b_recv,
    )
    def dn_wait(e, carry):
        for copy in dn_copies(e):
            copy.wait()
        return carry

    lax.fori_loop(0, chunks, dn_wait, 0)
    for copy in rec_moves:
        copy.wait()
    dn_out[...] = dn_home[...]
    rec_out[...] = rec_home[...]


def on_device(
    state_now, state_prev, courant_sq, reflectivity, direction, prev_gradient,
    residual, rec_depth, source_cell, wavelet, live_steps,
):
    shots, across, along = (lax.axis_size(a) for a in ("shot", "gx", "gy"))
    steps = residual.shape[1]
    extent_x, block_y, extent_z = courant_sq.shape
    rows, width = block_y // across, extent_x * across

    def turned(v):
        return jnp.transpose(v, (1, 0, 2))

    live = (lax.iota(jnp.int32, steps) < live_steps[0]).astype(jnp.float32)
    weighted = residual[0] * live[:, None, None]
    packed = jnp.concatenate([weighted, rec_depth.astype(jnp.float32)], axis=0)
    fit = 1
    while LANES // (2 * fit) > steps and rows % (2 * fit) == 0:
        fit *= 2
    pitch = LANES // fit
    chunks = rows
    while chunks > (steps - 1) // 2:
        chunks //= 2

    def gathered(v):
        v = jnp.pad(v, ((0, pitch - v.shape[0]), (0, 0), (0, 0)))
        v = v.reshape(pitch, extent_x, block_y // fit, fit)
        return jnp.transpose(v, (2, 1, 3, 0)).reshape(block_y // fit, extent_x, LANES)

    packed = gathered(packed)
    live_lanes = jnp.broadcast_to(jnp.tile(jnp.pad(live, (0, pitch - steps)), fit), (8, LANES))
    squares = jnp.sum(residual * residual)
    rr = jnp.pad(squares.reshape(1, 1), ((0, 7), (0, LANES - 1)))

    f32 = jnp.float32
    strip = (rows, width, extent_z)
    home = (block_y, extent_x, extent_z)
    grid = across * along
    dma = pltpu.SemaphoreType.DMA
    one = max(across - 1, 1)
    scratch = [
        pltpu.VMEM((steps + 1, rows + 4, 2, width, extent_z), f32),
        pltpu.VMEM((steps + 1, rows + 4, width, extent_z), f32),
        pltpu.VMEM((rows + 2, width, extent_z), f32),
        pltpu.VMEM(strip, f32),
        pltpu.VMEM(strip, f32),
        pltpu.VMEM((rows // fit + 2, width, LANES), f32),
        pltpu.VMEM((rows + 2, width, LANES), f32),
        pltpu.VMEM(strip, f32),
        pltpu.VMEM((shots - 1, rows // shots, width, extent_z), f32),
        pltpu.VMEM(strip, f32),
        pltpu.VMEM((rows + 2, width, extent_z), f32),
        pltpu.VMEM(strip, f32),
        pltpu.VMEM(home, f32),
        pltpu.VMEM((rows // fit, width, LANES), f32),
        pltpu.VMEM((block_y // fit, extent_x, LANES), f32),
        pltpu.VMEM((8, LANES), f32),
        pltpu.VMEM((grid, 8, LANES), f32),
        pltpu.VMEM((8, LANES), f32),
        pltpu.VMEM((shots * grid, 8, LANES), f32),
        dma((6,)), dma((4, one)), dma((4, one)), dma((2, one, chunks)), dma((2, one, chunks)),
        dma((steps + 1, 2)), dma((steps + 1, 2)), dma((steps + 1, 2)), dma((steps + 1, 2)), dma((4, 2)), dma((4, 2)),
        dma((shots - 1,)), dma((shots - 1,)), dma((shots - 1,)), dma((shots - 1,)),
        dma((across, chunks)), dma((one, chunks)), dma((across,)), dma((one,)),
        dma((grid - 1,)), dma((grid - 1,)), dma((shots * grid - 1,)), dma((shots * grid - 1,)),
    ]
    vmem, smem = pl.BlockSpec(memory_space=pltpu.VMEM), pl.BlockSpec(memory_space=pltpu.SMEM)
    dn, rec, stats, totals = pl.pallas_call(
        functools.partial(kernel, (shots, across, along, steps, fit, chunks)),
        out_shape=(
            jax.ShapeDtypeStruct(home, f32),
            jax.ShapeDtypeStruct((block_y // fit, extent_x, LANES), f32),
            jax.ShapeDtypeStruct((8, LANES), f32),
            jax.ShapeDtypeStruct((8, LANES), f32),
        ),
        in_specs=[smem, smem] + [vmem] * 8,
        out_specs=(vmem,) * 4,
        scratch_shapes=scratch,
        compiler_params=pltpu.CompilerParams(has_side_effects=True, vmem_limit_bytes=60 * 1024 * 1024),
        name="iteration",
    )(
        source_cell, wavelet, turned(state_now[0]), turned(state_prev[0]), turned(courant_sq),
        turned(direction), turned(prev_gradient), packed, live_lanes, rr,
    )
    sums = jnp.sum(stats, axis=1)
    ends = jnp.sum(totals, axis=1)
    beta = (sums[0] - sums[1]) / sums[2]
    slope = sums[0] + beta * sums[3]
    step = slope / ends[0]
    direction_next = turned(dn)
    image_next = reflectivity + step * direction_next
    rec = rec.reshape(block_y // fit, extent_x, fit, pitch)[..., :steps]
    records = jnp.transpose(rec, (3, 1, 0, 2)).reshape(steps, extent_x, block_y)
    residual_next = residual - step * records[None]
    entries = float(residual.size * shots * grid)
    misfit = ends[2] - 2.0 * step * ends[1] + step * step * ends[0]
    return image_next, direction_next, residual_next, 0.5 * misfit / entries


def solution(mesh):
    field, flat = P("shot", "gx", "gy", None), P("gx", "gy", None)
    traces = P("shot", None, "gx", "gy")
    return jax.shard_map(
        on_device,
        mesh=mesh,
        in_specs=(
            field, field, flat, flat, flat, flat, traces,
            P("shot", "gx", "gy"), P("shot", None), P("shot", None), P("shot"),
        ),
        out_specs=(flat, flat, traces, P()),
        check_vma=False,
    )
```

time: 187 us -> 152 us (0.81)
  Pallas kernels: 162 us -> 127 us
    pallas_call x1, Pallas kernels: 162 us -> 127 us  [on_device(): pl.pallas_call(functools.partial(kernel, (shots, across, along, steps, fi...]
    unnamed x21 -> x23, local copies, waits for them, and re-layouts: 4.96 us -> 4.78 us
where the time goes in v2:
time: 152 us
  Pallas kernels  127 us (84%)
  local copies, waits for them, and re-layouts  13.6 us (9%)
  between operations  8.51 us (6%)
  other arithmetic  3.03 us (2%)
    pallas_call x1, Pallas kernels, on_device(): pl.pallas_call(functools.partial(kernel, (shots, across, along, steps, fi...  127 us
    unnamed x23, local copies, waits for them, and re-layouts  4.78 us
    transpose x2, local copies, waits for them, and re-layouts, turned(): return jnp.transpose(v, (1, 0, 2))  4.44 us

profile of v2, /device:TPU:0, one launch (start us, length us, event | category | flops | bytes accessed | tf_op | source)
XLA Modules:
  0.0 151.7 jit_solution(11031502139269341152)
XLA Ops:
  0.6 0.0 copy-start.5
  0.6 0.0 copy-start.4
  0.7 2.9 %copy_bitcast_fusion = (f32[64,8,256]{2,1,0:T(8,128)}, f32[64,8,256]{2,1,0:T(8,128)}) fusion(f32[8,64,256]{2,1,0:T(8,128)} %param.16, f32[8,64,256]{2,1,0:T(8,128)} %param.15), kind=kLoop, calls=%fused_computation.1 | loop fusion | bytes 2097152 | tf_op jit(solution)/shard_map/transpose | solution.py:522
  3.5 0.0 copy-done.5
  3.5 0.0 copy-done.4
  3.5 1.6 %copy_bitcast_fusion.3 = (f32[64,8,256]{2,1,0:T(8,128)}, f32[64,8,256]{2,1,0:T(8,128)}) fusion(f32[1,8,64,256]{3,2,1,0:T(8,128)S(1)} %copy-done.4, f32[1,8,64,256]{3,2,1,0:T(8,128)S(1)} %copy-done.5), kind=kLoop, calls=%fused_computation.4 | loop fusion | bytes 2097152 | tf_op jit(solution)/shard_map/transpose | solution.py:522
  5.8 0.0 copy-start.8
  5.8 0.1 bitcast_multiply_fusion
  5.9 0.6 copy-done.8
  6.5 0.2 copy.44
  6.7 0.0 copy-start.2
  6.7 0.1 copy.45
  6.8 0.8 reshape.41.trace_ref
  7.6 0.1 tile.10
  7.7 0.6 broadcast_in_dim.4.live_ref
  8.3 1.1 copy.60
  9.4 0.6 multiply_reduce_fusion
  10.0 1.2 pad.14.rr_ref
  11.2 126.6 %iteration.1 = (f32[64,8,256]{2,1,0:T(8,128)}, f32[16,8,128]{2,1,0:T(8,128)}, f32[8,128]{1,0:T(8,128)}, f32[8,128]{1,0:T(8,128)}) custom-call(s32[1,3]{1,0:T(1,128)} %cell_ref.1, f32[1,15]{1,0:T(1,128)} %wave_ref.1, f32[64,8,256]{2,1,0:T(8,128)} %get-tuple-element.34.now_ref, f32[64,8,256]{2,1,0:T(8,128)} %get-tuple-element.33.prev_ref, ...), custom_call_target="tpu_custom_call" | custom-call | tf_op jit(solution)/shard_map/iteration/pallas_call | solution.py:578
  137.9 0.8 reduce_sum.28
  138.6 0.6 fusion.1
  141.2 0.0 copy-start.7
  142.5 0.1 reduce_sum.29
  142.7 0.6 fusion
  145.9 1.4 copy_add_fusion
  147.3 1.0 copy.49
  148.2 0.0 copy-done.6
  148.2 0.2 reshape.43
  148.4 0.2 copy.48
  148.7 0.8 copy.51
  149.4 0.2 copy-done
  149.6 1.0 copy.50
  (16 shorter events, 0.1 us)
Async XLA Ops:
  0.6 2.9 %copy-start.5 = (f32[1,8,64,256]{3,2,1,0:T(8,128)S(1)}, f32[1,8,64,256]{3,2,1,0:T(8,128)}, u32[]{:S(2)}) copy-start(f32[1,8,64,256]{3,2,1,0:T(8,128)} %param.11) | copy-start | bytes 1572868
  0.6 2.9 %copy-start.4 = (f32[1,8,64,256]{3,2,1,0:T(8,128)S(1)}, f32[1,8,64,256]{3,2,1,0:T(8,128)}, u32[]{:S(2)}) copy-start(f32[1,8,64,256]{3,2,1,0:T(8,128)} %param.12) | copy-start | bytes 1572868
  3.5 2.2 %copy-start.1 = (f32[1,16,8,64]{3,2,1,0:T(8,128)S(1)}, f32[1,16,8,64]{3,2,1,0:T(8,128)}, u32[]{:S(2)}) copy-start(f32[1,16,8,64]{3,2,1,0:T(8,128)} %param.17) | copy-start | bytes 98308
  5.8 0.7 copy-start.8
  6.7 1.6 %copy-start.2 = (f32[8,64,256]{2,1,0:T(8,128)S(1)}, f32[8,64,256]{2,1,0:T(8,128)}, u32[]{:S(2)}) copy-start(f32[8,64,256]{2,1,0:T(8,128)} %param.13) | copy-start | bytes 1572868
  11.2 134.7 %copy-start.3 = (f32[8,64,256]{2,1,0:T(8,128)S(1)}, f32[8,64,256]{2,1,0:T(8,128)}, u32[]{:S(2)}) copy-start(f32[8,64,256]{2,1,0:T(8,128)} %param.14) | copy-start | bytes 1572868
  141.2 1.3 copy-start.7
  147.3 1.0 copy-start.6
  148.6 1.0 copy-start
